TPU v7x, 32 devices: a whole 2x2x4 slice. The times are simulated.
32 devices in a mesh: gz: 32 (over z, y, x, core), vert: 1.
Axes of the slice: x: 2, y: 2, z: 4, core: 2. Of those that a mesh axis runs over, the one named last changes fastest.
Arguments:
- volume: float32 [256, 128, 1024], P('gz'), may hold values from -6 to 6
- angle_index: int32 [4], P('vert'), may hold values from 0 to 511
- detector_rows: int32 [128], replicated, may hold values from 0 to 127, each once
- measured: float32 [4, 128, 1024], P('vert', 'gz'), may hold values from -96 to 96
Outputs:
- residual: float32 [4, 128, 1024], P('vert', 'gz')
- gradient: float32 [256, 128, 1024], P('gz', 'vert')
All inputs are finite; a program needn't handle non-finite values.
Results may differ from a plain program's by a relative error of at most 0.0003.
Values sent between devices are 32-bit elements; how exact they have to be, the bound alone decides.
A program may use at most 64 MiB of HBM per device.

v0:
```python
import jax
import jax.numpy as jnp
from jax import lax
from jax.sharding import PartitionSpec as P

ANGLES = 512


def shifts(depth_pos, angle_value):
    slope_num = 2 * angle_value - ANGLES
    product = depth_pos * slope_num
    shift_whole = jnp.floor_divide(product, ANGLES)
    shift_part = (product - shift_whole * ANGLES).astype(jnp.float32) / ANGLES
    slope_value = slope_num.astype(jnp.float32) / ANGLES
    weight = jnp.sqrt(1.0 + slope_value * slope_value)
    return (shift_whole, shift_part, weight)


def backproject(back, angles, depth_pos, margin):
    columns, row_count = (back.shape[2], back.shape[1])
    back_cols = jnp.transpose(back, (0, 2, 1))
    back_pad = jnp.pad(back_cols, ((0, 0), (margin, margin), (0, 0)))

    def add_view(running, view_item):
        plane, angle_value = view_item
        shift_whole, shift_part, weight = shifts(depth_pos, angle_value)

        def add_shifted(offset, fraction):
            window = lax.dynamic_slice_in_dim(plane, offset, columns + 1, 0)
            return (1.0 - fraction) * window[1:, :] + fraction * window[:-1, :]

        contrib = jax.vmap(add_shifted)(margin - shift_whole - 1, shift_part)
        return (running + weight * contrib, None)

    start_sum = jnp.zeros((depth_pos.shape[0], columns, row_count), jnp.float32)
    summed, _ = lax.scan(add_view, start_sum, (back_pad, angles))
    return jnp.transpose(summed, (0, 2, 1))


def per_device(volume, angle_index, detector_rows, measured):
    layers, row_count, columns = volume.shape
    slab_count = lax.axis_size("gz")
    total_depth = layers * slab_count
    margin = total_depth // 2 + 2
    depth_pos = (
        lax.axis_index("gz") * layers + jnp.arange(layers, dtype=jnp.int32) - total_depth // 2
    )
    vol_cols = jnp.transpose(volume, (0, 2, 1))
    padded = jnp.pad(vol_cols, ((0, 0), (margin, margin), (0, 0)))

    def project(angle_value):
        shift_whole, shift_part, weight = shifts(depth_pos, angle_value)

        def project_shifted(plane, offset, fraction):
            window = lax.dynamic_slice_in_dim(plane, offset, columns + 1, 0)
            return (1.0 - fraction) * window[:-1, :] + fraction * window[1:, :]

        contrib = jax.vmap(project_shifted)(padded, margin + shift_whole, shift_part)
        return weight * jnp.sum(contrib, axis=0)

    partial_cols = lax.map(project, angle_index)
    det_cols = jnp.take(partial_cols, detector_rows, axis=2)
    det_order = jnp.transpose(det_cols, (0, 2, 1))
    res_scale = total_depth ** (-0.5)
    own_rows = lax.psum_scatter(det_order, "gz", scatter_dimension=1, tiled=True)
    residual = (own_rows - measured) * res_scale
    full_rows = lax.all_gather(residual, "gz", axis=1, tiled=True)
    back = jnp.zeros_like(full_rows).at[:, detector_rows, :].set(full_rows)
    view_scale = (angle_index.shape[0] * lax.axis_size("vert")) ** (-0.5)
    contrib_all = backproject(back, angle_index, depth_pos, margin)
    gradient = lax.psum_scatter(contrib_all, "vert", scatter_dimension=1, tiled=True) * view_scale
    return (residual, gradient)


def solution(mesh):
    in_specs = (P("gz", None, None), P("vert"), P(), P("vert", "gz", None))
    out_specs = (P("vert", "gz", None), P("gz", "vert", None))
    return jax.shard_map(
        per_device, mesh=mesh, in_specs=in_specs, out_specs=out_specs, check_vma=False
    )
```

profile of v0, /device:TPU:1, one launch (start us, length us, event | category | flops | bytes accessed | tf_op | source)
XLA Modules:
  0.0 543.9 jit_solution(5922922552793158404)
XLA Ops:
  8.5 5.3 copy.16
  13.9 4.8 pad.20
  18.7 191.6 %while.36 = (s32[]{:T(128)}, f32[4,1024,128]{1,0,2:T(4,128)}, s32[4]{0:T(128)S(1)}, f32[8,1284,128]{2,1,0:T(8,128)}, s32[]{:T(128)}, /*index=5*/s32[]{:T(128)}, ...) while((s32[]{:T(128)}, f32[4,1024,128]{1,0,2:T(4,128)}, ...), condition=%wide.region_2.3_spmd.clone, body=%wide.region_0.2_spmd.clone.sunk | while | flops 4194698 | bytes 13117662 | solution.py:61
  20.0 31.2 %while.39 = (s32[]{:T(128)}, f32[8,1284,128]{2,1,0:T(8,128)}, s32[8,3]{0,1:T(4,128)S(1)}, f32[8,1025,128]{2,1,0:T(8,128)}, s32[]{:T(128)}) while((s32[]{:T(128)}, f32[8,1284,128]{2,1,0:T(8,128)}, s32[8,3]{0,1:T(4,128)S(1)}, f32[8,1025,128]{2,1,0:T(8,128)}, s32[]{:T(128)}) %tuple.118), condition=%wide.while_cond, body=%wide.while_body.sunk | while | flops 2 | bytes 1058409 | solution.py:55
  40.1 3.3 dynamic-slice_dynamic-update-slice_fusion.2
  51.2 4.4 add_reduce_fusion.2
  56.1 10.5 %dynamic_update_slice.9 = f32[4,1024,128]{1,0,2:T(4,128)} dynamic-update-slice(f32[4,1024,128]{1,0,2:T(4,128)} %get-tuple-element.503, f32[1,1024,128]{1,0,2:T(1,128)S(1)} %copy.29, s32[]{:T(128)} %get-tuple-element.502, s32[]{:T(128)} %constant.246.clone.1..sunk, s32[]{:T(128)} %constant.246.clone.1..sunk) | dynamic-update-slice | bytes 1048580 | tf_op jit(solution)/shard_map/while/body/jit(dynamic_update_index_in_dim)/dynamic_update_slice | solution.py:61
  67.9 31.2 %while.39 = (s32[]{:T(128)}, f32[8,1284,128]{2,1,0:T(8,128)}, s32[8,3]{0,1:T(4,128)S(1)}, f32[8,1025,128]{2,1,0:T(8,128)}, s32[]{:T(128)}) while((s32[]{:T(128)}, f32[8,1284,128]{2,1,0:T(8,128)}, s32[8,3]{0,1:T(4,128)S(1)}, f32[8,1025,128]{2,1,0:T(8,128)}, s32[]{:T(128)}) %tuple.118), condition=%wide.while_cond, body=%wide.while_body.sunk | while | flops 2 | bytes 1058409 | solution.py:55
  88.0 3.3 dynamic-slice_dynamic-update-slice_fusion.2
  99.1 4.4 add_reduce_fusion.2
  104.0 10.5 %dynamic_update_slice.9 = f32[4,1024,128]{1,0,2:T(4,128)} dynamic-update-slice(f32[4,1024,128]{1,0,2:T(4,128)} %get-tuple-element.503, f32[1,1024,128]{1,0,2:T(1,128)S(1)} %copy.29, s32[]{:T(128)} %get-tuple-element.502, s32[]{:T(128)} %constant.246.clone.1..sunk, s32[]{:T(128)} %constant.246.clone.1..sunk) | dynamic-update-slice | bytes 1048580 | tf_op jit(solution)/shard_map/while/body/jit(dynamic_update_index_in_dim)/dynamic_update_slice | solution.py:61
  115.8 31.2 %while.39 = (s32[]{:T(128)}, f32[8,1284,128]{2,1,0:T(8,128)}, s32[8,3]{0,1:T(4,128)S(1)}, f32[8,1025,128]{2,1,0:T(8,128)}, s32[]{:T(128)}) while((s32[]{:T(128)}, f32[8,1284,128]{2,1,0:T(8,128)}, s32[8,3]{0,1:T(4,128)S(1)}, f32[8,1025,128]{2,1,0:T(8,128)}, s32[]{:T(128)}) %tuple.118), condition=%wide.while_cond, body=%wide.while_body.sunk | while | flops 2 | bytes 1058409 | solution.py:55
  147.0 4.4 add_reduce_fusion.2
  151.9 10.5 %dynamic_update_slice.9 = f32[4,1024,128]{1,0,2:T(4,128)} dynamic-update-slice(f32[4,1024,128]{1,0,2:T(4,128)} %get-tuple-element.503, f32[1,1024,128]{1,0,2:T(1,128)S(1)} %copy.29, s32[]{:T(128)} %get-tuple-element.502, s32[]{:T(128)} %constant.246.clone.1..sunk, s32[]{:T(128)} %constant.246.clone.1..sunk) | dynamic-update-slice | bytes 1048580 | tf_op jit(solution)/shard_map/while/body/jit(dynamic_update_index_in_dim)/dynamic_update_slice | solution.py:61
  163.7 31.2 %while.39 = (s32[]{:T(128)}, f32[8,1284,128]{2,1,0:T(8,128)}, s32[8,3]{0,1:T(4,128)S(1)}, f32[8,1025,128]{2,1,0:T(8,128)}, s32[]{:T(128)}) while((s32[]{:T(128)}, f32[8,1284,128]{2,1,0:T(8,128)}, s32[8,3]{0,1:T(4,128)S(1)}, f32[8,1025,128]{2,1,0:T(8,128)}, s32[]{:T(128)}) %tuple.118), condition=%wide.while_cond, body=%wide.while_body.sunk | while | flops 2 | bytes 1058409 | solution.py:55
  194.9 4.4 add_reduce_fusion.2
  199.8 10.5 %dynamic_update_slice.9 = f32[4,1024,128]{1,0,2:T(4,128)} dynamic-update-slice(f32[4,1024,128]{1,0,2:T(4,128)} %get-tuple-element.503, f32[1,1024,128]{1,0,2:T(1,128)S(1)} %copy.29, s32[]{:T(128)} %get-tuple-element.502, s32[]{:T(128)} %constant.246.clone.1..sunk, s32[]{:T(128)} %constant.246.clone.1..sunk) | dynamic-update-slice | bytes 1048580 | tf_op jit(solution)/shard_map/while/body/jit(dynamic_update_index_in_dim)/dynamic_update_slice | solution.py:61
  210.4 3.4 gather_fusion
  215.7 135.6 %all-reduce.7.cloned.1.call-done = f32[4,128,1024]{2,0,1:T(4,128)} async-done(((f32[4,128,1024]{2,0,1:T(4,128)}), f32[4,128,1024]{2,0,1:T(4,128)}) %all-reduce.7.cloned.1.call-update) | async-done | bytes 2097168
  354.3 56.4 %all-gather.2.cloned.1.call-done = f32[4,128,1024]{2,0,1:T(4,128)} async-done(((f32[4,4,1024]{2,0,1:T(4,128)}), f32[4,128,1024]{2,0,1:T(4,128)}) %all-gather.2.cloned.1.call-update) | async-done | bytes 2097168 | tf_op jit(solution)/shard_map/all_gather | solution.py:67
  411.2 11.8 %scatter_fusion = f32[4,128,1024]{2,0,1:T(4,128)S(1)} fusion(f32[4,128,1024]{2,0,1:T(4,128)S(1)} %broadcast_in_dim.35, s32[128]{0:T(128)S(1)} %compare_select_fusion.14, f32[128,4,1024]{2,1,0:T(4,128)} %bitcast.60), kind=kCustom, calls=%fused_computation.1 | custom fusion | bytes 6291968 | tf_op jit(solution)/shard_map/scatter | solution.py:68
  426.7 99.9 %while.38 = (s32[]{:T(128)}, f32[8,1024,128]{2,1,0:T(8,128)}, s32[4]{0:T(128)S(1)}, f32[4,1284,128]{2,1,0:T(8,128)S(1)}, s32[]{:T(128)}, /*index=5*/s32[]{:T(128...) while((s32[]{:T(128)}, f32[8,1024,128]{2,1,0:T(8,128)}, ...), condition=%wide.region_6.7_spmd.clone, body=%wide.region_5.6_spmd.clone.sunk | while | flops 6291827 | bytes 19146876 | solution.py:36
  428.0 16.1 %while.40 = (s32[]{:T(128)}, f32[1284,128]{1,0:T(8,128)S(1)}, s32[8,2]{0,1:T(2,128)S(1)}, f32[8,1025,128]{2,1,0:T(8,128)}, s32[]{:T(128)}) while((s32[]{:T(128)}, f32[1284,128]{1,0:T(8,128)S(1)}, s32[8,2]{0,1:T(2,128)S(1)}, f32[8,1025,128]{2,1,0:T(8,128)}, s32[]{:T(128)}) %tuple.115), condition=%wide.while_cond.1, body=%wide.while_body.1.sunk | while | flops 2 | bytes 1054297 | solution.py:29
  444.2 6.6 %select_add_fusion.2 = f32[8,1024,128]{2,1,0:T(8,128)} fusion(f32[8,1024,128]{2,1,0:T(8,128)} %get-tuple-element.539, f32[8,1025,128]{2,1,0:T(8,128)} %get-tuple-element.446, f32[8]{0:T(128)S(1)} %get-tuple-element.447, f32[8]{0:T(128)S(1)} %get-tuple-element.448, f32[]{:T(128)S(6)} %sqrt.21, pred[]{:T(512)S(6)} %compare.81), kind=kLoop, calls=%fused_computation.24.clone.1 | loop fusion | flops 6291456 | bytes 16777284 | tf_op jit(solution)/shard_map/while/body/eval_jaxpr/add | solution.py:33
  452.1 16.1 %while.40 = (s32[]{:T(128)}, f32[1284,128]{1,0:T(8,128)S(1)}, s32[8,2]{0,1:T(2,128)S(1)}, f32[8,1025,128]{2,1,0:T(8,128)}, s32[]{:T(128)}) while((s32[]{:T(128)}, f32[1284,128]{1,0:T(8,128)S(1)}, s32[8,2]{0,1:T(2,128)S(1)}, f32[8,1025,128]{2,1,0:T(8,128)}, s32[]{:T(128)}) %tuple.115), condition=%wide.while_cond.1, body=%wide.while_body.1.sunk | while | flops 2 | bytes 1054297 | solution.py:29
  468.3 7.8 %select_add_fusion.2 = f32[8,1024,128]{2,1,0:T(8,128)} fusion(f32[8,1024,128]{2,1,0:T(8,128)} %get-tuple-element.539, f32[8,1025,128]{2,1,0:T(8,128)} %get-tuple-element.446, f32[8]{0:T(128)S(1)} %get-tuple-element.447, f32[8]{0:T(128)S(1)} %get-tuple-element.448, f32[]{:T(128)S(6)} %sqrt.21, pred[]{:T(512)S(6)} %compare.81), kind=kLoop, calls=%fused_computation.24.clone.1 | loop fusion | flops 6291456 | bytes 16777284 | tf_op jit(solution)/shard_map/while/body/eval_jaxpr/add | solution.py:33
  477.3 16.1 %while.40 = (s32[]{:T(128)}, f32[1284,128]{1,0:T(8,128)S(1)}, s32[8,2]{0,1:T(2,128)S(1)}, f32[8,1025,128]{2,1,0:T(8,128)}, s32[]{:T(128)}) while((s32[]{:T(128)}, f32[1284,128]{1,0:T(8,128)S(1)}, s32[8,2]{0,1:T(2,128)S(1)}, f32[8,1025,128]{2,1,0:T(8,128)}, s32[]{:T(128)}) %tuple.115), condition=%wide.while_cond.1, body=%wide.while_body.1.sunk | while | flops 2 | bytes 1054297 | solution.py:29
  493.6 7.8 %select_add_fusion.2 = f32[8,1024,128]{2,1,0:T(8,128)} fusion(f32[8,1024,128]{2,1,0:T(8,128)} %get-tuple-element.539, f32[8,1025,128]{2,1,0:T(8,128)} %get-tuple-element.446, f32[8]{0:T(128)S(1)} %get-tuple-element.447, f32[8]{0:T(128)S(1)} %get-tuple-element.448, f32[]{:T(128)S(6)} %sqrt.21, pred[]{:T(512)S(6)} %compare.81), kind=kLoop, calls=%fused_computation.24.clone.1 | loop fusion | flops 6291456 | bytes 16777284 | tf_op jit(solution)/shard_map/while/body/eval_jaxpr/add | solution.py:33
  502.6 16.1 %while.40 = (s32[]{:T(128)}, f32[1284,128]{1,0:T(8,128)S(1)}, s32[8,2]{0,1:T(2,128)S(1)}, f32[8,1025,128]{2,1,0:T(8,128)}, s32[]{:T(128)}) while((s32[]{:T(128)}, f32[1284,128]{1,0:T(8,128)S(1)}, s32[8,2]{0,1:T(2,128)S(1)}, f32[8,1025,128]{2,1,0:T(8,128)}, s32[]{:T(128)}) %tuple.115), condition=%wide.while_cond.1, body=%wide.while_body.1.sunk | while | flops 2 | bytes 1054297 | solution.py:29
  518.8 7.8 %select_add_fusion.2 = f32[8,1024,128]{2,1,0:T(8,128)} fusion(f32[8,1024,128]{2,1,0:T(8,128)} %get-tuple-element.539, f32[8,1025,128]{2,1,0:T(8,128)} %get-tuple-element.446, f32[8]{0:T(128)S(1)} %get-tuple-element.447, f32[8]{0:T(128)S(1)} %get-tuple-element.448, f32[]{:T(128)S(6)} %sqrt.21, pred[]{:T(512)S(6)} %compare.81), kind=kLoop, calls=%fused_computation.24.clone.1 | loop fusion | flops 6291456 | bytes 16777284 | tf_op jit(solution)/shard_map/while/body/eval_jaxpr/add | solution.py:33
  526.7 5.4 copy.20
  532.0 5.0 multiply_bitcast_fusion.1
  (265 shorter events, 200.1 us)
Async XLA Ops:
  7.2 344.1 %all-reduce.7.cloned.1.call-start = ((), (), s32[]{:S(2)}) async-start(), calls=%async_computation.1 | async-start | bytes 4194304
  13.9 4.8 copy-start.1
  213.8 137.5 %copy-start = (f32[4,4,1024]{2,1,0:T(4,128)S(1)}, f32[4,4,1024]{2,1,0:T(4,128)}, u32[]{:S(2)}) copy-start(f32[4,4,1024]{2,1,0:T(4,128)} %param.11) | copy-start | bytes 196612
  215.6 195.1 %all-gather.2.cloned.1.call-start = ((), (), s32[]{:S(2)}) async-start(), calls=%async_computation | async-start | bytes 2162688 | tf_op jit(solution)/shard_map/all_gather | solution.py:67
Sparse Core Ops, SparseCore 0:
  215.8 135.4 all-reduce.6
  354.1 56.5 all-gather.1
where the time goes:
time: 548 us; the launch traced here: 544 us
  local copies, waits for them, and re-layouts  274 us (50%)
  waiting for transfers between devices  192 us (35%)
  other arithmetic  57.8 us (11%)
  between operations  14.1 us (3%)
  loops' own time  5.8 us (1%)
    gather x192, local copies, waits for them, and re-layouts  189 us
    unnamed x3, waiting for transfers between devices  136 us
    all_gather x1, waiting for transfers between devices, per_device(): full_rows = lax.all_gather(residual, 'gz', axis=1, tiled=True)  56.4 us
    dynamic_update_slice x8, local copies, waits for them, and re-layouts, per_device(): partial_cols = lax.map(project, angle_index)  43.7 us
    add x4, other arithmetic, add_view(): return (running + weight * contrib, None)  30.1 us
    reduce_sum x4, other arithmetic, project(): return weight * jnp.sum(contrib, axis=0)  17.6 us
    scatter x1, local copies, waits for them, and re-layouts, per_device(): back = jnp.zeros_like(full_rows).at[:, detector_rows, :].set(full_rows)  11.8 us
  transfers between devices with their start and end apart: 2, of which 2 were waited for; matrix products, arithmetic and copies ran while one was open for 0% of the time, Pallas kernels for 0%

commit v1 on v0

v1 whole, which is shorter than its diff:
```python
import functools

import jax
import jax.numpy as jnp
from jax import lax
from jax.experimental import pallas as pl
from jax.experimental.pallas import tpu as pltpu
from jax.sharding import PartitionSpec as P

ANGLES = 512
LANES = 128
SUBLANES = 8
COLUMN_PARTS = 2
MESH = pl.DeviceIdType.MESH


def layer_steps(angle, base, layers):
    slope_num = 2 * angle - ANGLES
    rising = slope_num >= 0
    bits = ANGLES.bit_length() - 1
    steps = []
    for i in range(layers):
        layer = jnp.where(rising, i, layers - 1 - i)
        product = (base + layer) * slope_num
        whole = lax.shift_right_arithmetic(product, jnp.int32(bits))
        fraction = (product - whole * ANGLES).astype(jnp.float32) * (1.0 / ANGLES)
        steps.append((layer, whole, fraction))
    return steps


def one_hot_dot(one_hot, values):
    high = values.astype(jnp.bfloat16)
    low = (values - high.astype(jnp.float32)).astype(jnp.bfloat16)
    dot = functools.partial(jnp.dot, preferred_element_type=jnp.float32)
    return dot(one_hot, high) + dot(one_hot, low)


def project_kernel(base_ref, angle_ref, weight_ref, target_ref, vol_ref, out_ref, xs, dxs, partial):
    layers, block_rows, columns = vol_ref.shape
    views, row_count, _ = partial.shape
    width = xs.shape[2]
    step = pl.program_id(0)
    base = base_ref[0]

    def row_group(group, carry):
        rows = pl.ds(pl.multiple_of(group * SUBLANES, SUBLANES), SUBLANES)
        pad = jnp.zeros((SUBLANES, width - columns), jnp.float32)
        for layer in range(layers):
            plane = jnp.concatenate([vol_ref[layer, rows, :], pad], axis=1)
            xs[layer] = plane
            dxs[layer] = pltpu.roll(plane, width - 1, 1) - plane
        for view in range(views):
            steps = layer_steps(angle_ref[view], base, layers)
            total = None
            for i in reversed(range(layers)):
                layer, whole, fraction = steps[i]
                lerp = xs[layer] + fraction * dxs[layer]
                if total is None:
                    total = lerp
                else:
                    moved = steps[i + 1][1] - whole
                    total = lerp + jnp.where(moved == 1, pltpu.roll(total, width - 1, 1), total)
            first = steps[0][1]
            shift = jnp.where(first > 0, width - first, -first)
            total = pltpu.roll(total, shift, 1)[:, :columns] * weight_ref[view]
            out_rows = pl.ds(pl.multiple_of(step * block_rows + group * SUBLANES, SUBLANES), SUBLANES)
            partial[view, out_rows, :] = total
        return carry

    lax.fori_loop(0, block_rows // SUBLANES, row_group, 0)

    @pl.when(step == pl.num_programs(0) - 1)
    def _():
        groups = target_ref.shape[0]
        each = views // groups
        parts = out_ref.shape[0] // groups
        part_columns = columns // parts
        for group in range(groups):
            count = target_ref.shape[1]
            source = lax.broadcasted_iota(jnp.int32, (count, each * row_count), 1)
            one_hot = (target_ref[group] == source).astype(jnp.float32).astype(jnp.bfloat16)
            for part in range(parts):
                values = partial[
                    group * each : (group + 1) * each, :, part * part_columns : (part + 1) * part_columns
                ].reshape(each * row_count, part_columns)
                moved = one_hot_dot(one_hot, values)
                out_ref[group * parts + part] = moved.reshape(out_ref.shape[1:])


def backproject_kernel(base_ref, angle_ref, weight_ref, target_ref, full_ref, out_ref, back):
    layers, block_rows, columns = out_ref.shape
    views, row_count, width = back.shape
    step = pl.program_id(0)
    base = base_ref[0]

    @pl.when(step == 0)
    def _():
        groups = target_ref.shape[0]
        each = views // groups
        parts = full_ref.shape[0] // groups
        part_columns = columns // parts
        for view in range(views):
            back[view, :, columns:] = jnp.zeros((row_count, width - columns), jnp.float32)
        for group in range(groups):
            count = target_ref.shape[2]
            source = lax.broadcasted_iota(jnp.int32, (each * row_count, count), 0)
            one_hot = (target_ref[group] == source).astype(jnp.float32).astype(jnp.bfloat16)
            for part in range(parts):
                values = full_ref[group * parts + part].reshape(count, part_columns)
                moved = one_hot_dot(one_hot, values).reshape(each, row_count, part_columns)
                for i in range(each):
                    view = group * each + i
                    back[view, :, part * part_columns : (part + 1) * part_columns] = (
                        moved[i] * weight_ref[view]
                    )

    def row_group(group, carry):
        rows = pl.ds(pl.multiple_of(group * SUBLANES, SUBLANES), SUBLANES)
        back_rows = pl.ds(pl.multiple_of(step * block_rows + group * SUBLANES, SUBLANES), SUBLANES)
        for view in range(views):
            steps = layer_steps(angle_ref[view], base, layers)
            first = steps[0][1]
            shift = jnp.where(first < 0, width + first, first)
            current = pltpu.roll(back[view, back_rows, :], shift, 1)
            for i in range(layers):
                layer, whole, fraction = steps[i]
                after = pltpu.roll(current, 1, 1)
                contrib = (current + fraction * (after - current))[:, :columns]
                if view == 0:
                    out_ref[layer, rows, :] = contrib
                else:
                    out_ref[layer, rows, :] += contrib
                if i + 1 < layers:
                    current = jnp.where(steps[i + 1][1] - whole == 1, after, current)
        return carry

    lax.fori_loop(0, block_rows // SUBLANES, row_group, 0)


def exchange_kernel(n, orders, scale, in_ref, meas_ref, res_ref, full_ref,
                    got0, got1, got2, got3, put1, put2, put3, send_sem, recv_sem):
    me = lax.axis_index("gz")
    high_count = n // 8
    core, bit1, bit2, high = me % 2, (me // 2) % 2, (me // 4) % 2, me // 8
    other_core = me + 1 - 2 * core
    other1, other2 = me + 2 - 4 * bit1, me + 4 - 8 * bit2
    others = [me + 8 * (lax.rem(high + j, high_count) - high) for j in range(1, high_count)]
    count = in_ref.shape[0]
    part_columns = in_ref.shape[-1]
    per_group = count // meas_ref.shape[0]

    barrier = pltpu.get_barrier_semaphore()
    for peer in [other_core, other1, other2] + others:
        pl.semaphore_signal(barrier, inc=1, device_id={"gz": peer}, device_id_type=MESH)
    pl.semaphore_wait(barrier, 3 + len(others))

    started = {}

    def start(part, stage, source, target, peer):
        copy = pltpu.make_async_remote_copy(
            src_ref=source, dst_ref=target,
            send_sem=send_sem.at[part, stage], recv_sem=recv_sem.at[part, stage],
            device_id={"gz": peer}, device_id_type=MESH,
        )
        copy.start()
        started[part, stage] = copy

    def arrived(part, stage):
        started[part, stage].wait_recv()

    def ends(part):
        if orders[part] == 0:
            return bit1, bit2, other1, other2
        return bit2, bit1, other2, other1

    parts = range(count)
    for part in parts:
        start(part, 0, in_ref.at[part, 1 - core], got0.at[part], other_core)
    for part in parts:
        a, b, peer_a, peer_b = ends(part)
        arrived(part, 0)
        put1[part] = in_ref[part, core, 1 - a] + got0[part, 1 - a]
        start(part, 1, put1.at[part], got1.at[part], peer_a)
    for part in parts:
        a, b, peer_a, peer_b = ends(part)
        arrived(part, 1)
        put2[part] = in_ref[part, core, a, 1 - b] + got0[part, a, 1 - b] + got1[part, 1 - b]
        start(part, 2, put2.at[part], got2.at[part], peer_b)
    for part in parts:
        a, b, peer_a, peer_b = ends(part)
        arrived(part, 2)
        put3[part] = in_ref[part, core, a, b] + got0[part, a, b] + got1[part, b] + got2[part]
        for j, peer in enumerate(others):
            start(part, 3 + j, put3.at[part, lax.rem(high + j + 1, high_count)], got3.at[part, j], peer)
    gather = 3 + len(others)
    for part in parts:
        a, b, peer_a, peer_b = ends(part)
        total = put3[part, high]
        for j in range(len(others)):
            arrived(part, 3 + j)
            total = total + got3[part, j]
        group, column = part // per_group, (part % per_group) * part_columns
        residual = (total - meas_ref[group, :, column : column + part_columns]) * scale
        res_ref[group, :, column : column + part_columns] = residual
        full_ref[part, core, a, b, high] = residual
        mine = full_ref.at[part, core, a, b, high]
        for j, peer in enumerate(others):
            start(part, gather + j, mine, mine, peer)
    last = gather + len(others)
    for part in parts:
        a, b, peer_a, peer_b = ends(part)
        for j in range(len(others)):
            arrived(part, gather + j)
        mine = full_ref.at[part, core, a, b]
        start(part, last, mine, mine, peer_b)
    for part in parts:
        a, b, peer_a, peer_b = ends(part)
        arrived(part, last)
        mine = full_ref.at[part, core, a]
        start(part, last + 1, mine, mine, peer_a)
    for part in parts:
        arrived(part, last + 1)
        mine = full_ref.at[part, core]
        start(part, last + 2, mine, mine, other_core)
    for part in parts:
        arrived(part, last + 2)
    for copy in started.values():
        copy.wait_send()


def per_device(volume, angle_index, detector_rows, measured):
    layers, row_count, columns = volume.shape
    views = angle_index.shape[0]
    n = lax.axis_size("gz")
    total_depth = layers * n
    own_rows = row_count // n
    each = SUBLANES // own_rows
    groups = views // each
    high_count = n // 8
    margin = -(-(total_depth // 2) // LANES) * LANES
    width = columns + 2 * margin
    part_columns = columns // COLUMN_PARTS
    count = groups * COLUMN_PARTS
    orders = tuple((part // COLUMN_PARTS) % 2 for part in range(count))
    block_rows = 32
    res_scale = total_depth ** (-0.5)
    view_scale = (views * lax.axis_size("vert")) ** (-0.5)

    base = (lax.axis_index("gz") * layers - total_depth // 2).astype(jnp.int32).reshape(1)
    slope = (2 * angle_index - ANGLES).astype(jnp.float32) / ANGLES
    weight = jnp.sqrt(1.0 + slope * slope)

    by_bits = detector_rows.reshape(high_count, 2, 2, 2, own_rows)
    targets = []
    for group in range(groups):
        order = (3, 2, 1, 0, 4) if group % 2 == 0 else (3, 1, 2, 0, 4)
        placed = jnp.transpose(by_bits, order).reshape(n, 1, own_rows)
        placed = placed + (jnp.arange(each, dtype=jnp.int32) * row_count)[None, :, None]
        targets.append(placed.reshape(-1))
    target = jnp.stack(targets)

    smem = pl.BlockSpec(memory_space=pltpu.SMEM)
    vmem = pl.BlockSpec(memory_space=pltpu.VMEM)
    full_shape = (count, 2, 2, 2, high_count, SUBLANES, part_columns)
    half = (SUBLANES, part_columns)
    whole = pl.BlockSpec(full_shape, lambda i: (0,) * len(full_shape))
    partials = pl.pallas_call(
        project_kernel,
        grid=(row_count // block_rows,),
        out_shape=jax.ShapeDtypeStruct(full_shape, jnp.float32),
        in_specs=[
            smem, smem, smem,
            pl.BlockSpec((groups, target.shape[1], 1), lambda i: (0, 0, 0)),
            pl.BlockSpec((layers, block_rows, columns), lambda i: (0, i, 0)),
        ],
        out_specs=whole,
        scratch_shapes=[
            pltpu.VMEM((layers, SUBLANES, width), jnp.float32),
            pltpu.VMEM((layers, SUBLANES, width), jnp.float32),
            pltpu.VMEM((views, row_count, columns), jnp.float32),
        ],
        name="project",
    )(base, angle_index, weight, target[:, :, None], volume)

    others = high_count - 1
    stages = 6 + 2 * others
    residual, full = pl.pallas_call(
        functools.partial(exchange_kernel, n, orders, res_scale),
        out_shape=(
            jax.ShapeDtypeStruct((groups, SUBLANES, columns), jnp.float32),
            jax.ShapeDtypeStruct(full_shape, jnp.float32),
        ),
        in_specs=[vmem, vmem],
        out_specs=(vmem, vmem),
        scratch_shapes=[
            pltpu.VMEM((count, 2, 2, high_count) + half, jnp.float32),
            pltpu.VMEM((count, 2, high_count) + half, jnp.float32),
            pltpu.VMEM((count, high_count) + half, jnp.float32),
            pltpu.VMEM((count, others) + half, jnp.float32),
            pltpu.VMEM((count, 2, high_count) + half, jnp.float32),
            pltpu.VMEM((count, high_count) + half, jnp.float32),
            pltpu.VMEM((count, high_count) + half, jnp.float32),
            pltpu.SemaphoreType.DMA((count, stages)),
            pltpu.SemaphoreType.DMA((count, stages)),
        ],
        compiler_params=pltpu.CompilerParams(collective_id=0, has_side_effects=True),
        name="exchange",
    )(partials, measured.reshape(groups, SUBLANES, columns))

    gradient = pl.pallas_call(
        backproject_kernel,
        grid=(row_count // block_rows,),
        out_shape=jax.ShapeDtypeStruct((layers, row_count, columns), jnp.float32),
        in_specs=[
            smem, smem, smem,
            pl.BlockSpec((groups, 1, target.shape[1]), lambda i: (0, 0, 0)),
            whole,
        ],
        out_specs=pl.BlockSpec((layers, block_rows, columns), lambda i: (0, i, 0)),
        scratch_shapes=[pltpu.VMEM((views, row_count, width), jnp.float32)],
        name="backproject",
    )(base, angle_index, weight * view_scale, target[:, None, :], full)
    gradient = lax.psum_scatter(gradient, "vert", scatter_dimension=1, tiled=True)
    return (residual.reshape(measured.shape), gradient)


def solution(mesh):
    in_specs = (P("gz", None, None), P("vert"), P(), P("vert", "gz", None))
    out_specs = (P("vert", "gz", None), P("gz", "vert", None))
    return jax.shard_map(
        per_device, mesh=mesh, in_specs=in_specs, out_specs=out_specs, check_vma=False
    )
```

time: 548 us -> 87.9 us (0.16)
  local copies, waits for them, and re-layouts: 274 us -> 5.42 us
  waiting for transfers between devices: 192 us -> 0 us
  Pallas kernels: 0 us -> 80 us
  other arithmetic: 57.8 us -> 1.36 us
  between operations: 14.1 us -> 0.69 us
  loops' own time: 5.8 us -> 0 us
    gather x193 -> x0, local copies, waits for them, and re-layouts: 193 us -> none
    unnamed x3 -> x0, waiting for transfers between devices: 136 us -> none
    pallas_call x0 -> x3, Pallas kernels: none -> 80 us  [the longest x1 44.3 us: per_device(): pl.pallas_call(functools.partial(exchange_kernel, n, orders, res_scale),...]
    all_gather x1 -> x0, waiting for transfers between devices: 56.4 us -> none  [per_device(): full_rows = lax.all_gather(residual, 'gz', axis=1, tiled=True)]
    dynamic_update_slice x8 -> x0, local copies, waits for them, and re-layouts: 43.7 us -> none  [per_device(): partial_cols = lax.map(project, angle_index)]
    add x4 -> x1, other arithmetic: 30.1 us -> 0.09 us  [per_device(): placed + (jnp.arange(each, dtype=jnp.int32) * row_count)[None, :, None]]
    reduce_sum x4 -> x0, other arithmetic: 17.6 us -> none  [project(): return weight * jnp.sum(contrib, axis=0)]
    scatter x1 -> x0, local copies, waits for them, and re-layouts: 11.8 us -> none  [per_device(): back = jnp.zeros_like(full_rows).at[:, detector_rows, :].set(full_rows)]
  transfers between devices with their start and end apart: 2 -> 0, of which waited for: 2 -> 0; matrix products, arithmetic and copies ran while one was open for 0% -> 0% of each run, Pallas kernels for 0% -> 0%
where the time goes in v1:
time: 87.9 us; the launch traced here: 87.5 us
  Pallas kernels  80 us (91%)
  local copies, waits for them, and re-layouts  5.42 us (6%)
  other arithmetic  1.36 us (2%)
    pallas_call x1, Pallas kernels, per_device(): pl.pallas_call(functools.partial(exchange_kernel, n, orders, res_scale),...  44.3 us
    pallas_call x1, Pallas kernels, per_device(): pl.pallas_call(backproject_kernel, grid=(row_count // block_rows,), out_s...  19.5 us
    pallas_call x1, Pallas kernels, per_device(): pl.pallas_call(project_kernel, grid=(row_count // block_rows,), out_shape...  16.1 us

profile of v1, /device:TPU:1, one launch (start us, length us, event | category | flops | bytes accessed | tf_op | source)
XLA Modules:
  0.0 87.5 jit_solution(17994575309815226264)
XLA Ops:
  0.6 1.3 %broadcast_multiply_fusion = (f32[4]{0:T(128)}, f32[4]{0:T(128)}) fusion(s32[4]{0:T(128)} %angle_ref.3), kind=kLoop, calls=%fused_computation.5 | loop fusion | flops 28 | bytes 48 | tf_op jit(solution)/shard_map/mul | solution.py:322
  1.9 0.8 reshape.69
  2.7 0.1 broadcast_add_fusion.1
  2.8 0.1 add.61
  2.9 0.1 add.65
  3.0 0.6 broadcast_in_dim.9.target_ref
  3.6 1.5 %reshape.70.meas_ref = f32[2,8,1024]{2,1,0:T(8,128)} reshape(f32[4,4,1024]{2,1,0:T(4,128)} %param.7) | data formatting | bytes 131072 | tf_op jit(solution)/shard_map/reshape | solution.py:308
  5.1 0.8 copy.15.target_ref
  6.0 16.1 %project.1.in_ref = f32[4,2,2,2,4,8,512]{6,5,4,3,2,1,0:T(8,128)} custom-call(s32[1]{0:T(128)} %bitcast.base_ref, s32[4]{0:T(128)} %angle_ref.3, f32[4]{0:T(128)} %get-tuple-element.7.weight_ref, s32[2,256,1]{2,1,0:T(8,128)} %copy.15.target_ref, f32[8,128,1024]{2,1,0:T(8,128)} %vol_ref.1), custom_call_target="tpu_custom_call" | custom-call | tf_op jit(solution)/shard_map/project/pallas_call | solution.py:267
  22.1 44.3 %exchange.1 = (f32[2,8,1024]{2,1,0:T(8,128)}, f32[4,2,2,2,4,8,512]{6,5,4,3,2,1,0:T(8,128)}) custom-call(f32[4,2,2,2,4,8,512]{6,5,4,3,2,1,0:T(8,128)} %project.1.in_ref, f32[2,8,1024]{2,1,0:T(8,128)} %reshape.70.meas_ref), custom_call_target="tpu_custom_call" | custom-call | tf_op jit(solution)/shard_map/exchange/pallas_call | solution.py:287
  66.5 1.5 %reshape.71 = f32[4,4,1024]{2,1,0:T(4,128)} reshape(f32[2,8,1024]{2,1,0:T(8,128)} %get-tuple-element.4) | data formatting | bytes 131072 | tf_op jit(solution)/shard_map/reshape | solution.py:324
  67.9 19.5 %backproject.1 = f32[8,128,1024]{2,1,0:T(8,128)} custom-call(s32[1]{0:T(128)} %bitcast.base_ref, s32[4]{0:T(128)} %angle_ref.3, f32[4]{0:T(128)} %get-tuple-element.6.weight_ref, s32[2,1,256]{2,1,0:T(1,128)} %broadcast_in_dim.9.target_ref, f32[4,2,2,2,4,8,512]{6,5,4,3,2,1,0:T(8,128)} %get-tuple-element.5.full_ref), custom_call_target="tpu_custom_call" | custom-call | tf_op jit(solution)/shard_map/backproject/pallas_call | solution.py:310
  (4 shorter events, 0.0 us)

commit v2 on v1

v2 whole, which is shorter than its diff:
```python
import functools

import jax
import jax.numpy as jnp
from jax import lax
from jax.experimental import pallas as pl
from jax.experimental.pallas import tpu as pltpu
from jax.sharding import PartitionSpec as P

ANGLES = 512
LANES = 128
SUBLANES = 8
COLUMN_PARTS = 2
CHUNK = 64
MESH = pl.DeviceIdType.MESH


def log2(value):
    return value.bit_length() - 1


def shift_parts(depth, angle):
    product = depth * (2 * angle - ANGLES)
    whole = lax.shift_right_arithmetic(product, jnp.int32(log2(ANGLES)))
    fraction = (product - whole * ANGLES).astype(jnp.float32) * (1.0 / ANGLES)
    return whole, fraction


def ray_weight(angle):
    slope = (2 * angle - ANGLES).astype(jnp.float32) * (1.0 / ANGLES)
    return jnp.sqrt(jnp.full((1, LANES), 1.0 + slope * slope, jnp.float32))


def row_places(det_ref, n, each, own_rows, order):
    row_count = det_ref.shape[1]
    count = n * each * own_rows
    place = lax.broadcasted_iota(jnp.int32, (count, row_count), 0)
    detector = lax.broadcasted_iota(jnp.int32, (count, row_count), 1)
    row = place & (own_rows - 1)
    view = lax.shift_right_logical(place, log2(own_rows)) & (each - 1)
    slot = lax.shift_right_logical(place, log2(own_rows * each))
    high_count = n // 8
    high = slot & (high_count - 1)
    bits = lax.shift_right_logical(slot, log2(high_count))
    second, first, core = bits & 1, lax.shift_right_logical(bits, 1) & 1, lax.shift_right_logical(bits, 2)
    bit1, bit2 = (first, second) if order == 0 else (second, first)
    owner = high * 8 + bit2 * 4 + bit1 * 2 + core
    from_detector = (owner * own_rows + row) == detector
    volume_row = lax.broadcasted_iota(jnp.int32, (row_count, row_count), 0)
    records = (det_ref[...] == volume_row).astype(jnp.float32).astype(jnp.bfloat16)
    places = []
    for i in range(each):
        pick = (from_detector & (view == i)).astype(jnp.float32).astype(jnp.bfloat16)
        moved = lax.dot_general(pick, records, (((1,), (1,)), ((), ())), preferred_element_type=jnp.float32)
        places.append(moved.astype(jnp.bfloat16))
    return places


def two_terms(values):
    high = values.astype(jnp.bfloat16)
    return high, (values - high.astype(jnp.float32)).astype(jnp.bfloat16)


def place_dot(a, b, dims):
    return lax.dot_general(a, b, (dims, ((), ())), preferred_element_type=jnp.float32)


def project_kernel(n, total_depth, angle_ref, det_ref, vol_ref, out_ref, planes, partial):
    layers, height, _ = planes.shape
    views, columns, row_count = partial.shape
    margin = (height - columns) // 2
    layer = pl.program_id(0)
    base = lax.axis_index("gz") * layers - total_depth // 2

    blank = jnp.zeros((margin, row_count), jnp.float32)
    planes[layer, :margin, :] = blank
    planes[layer, margin + columns :, :] = blank
    for column in range(0, columns, LANES):
        planes[layer, margin + column : margin + column + LANES, :] = vol_ref[0, :, column : column + LANES].T

    @pl.when(layer == layers - 1)
    def _():
        for view in range(views):
            steps = [shift_parts(base + i, angle_ref[view]) for i in range(layers)]
            weight = ray_weight(angle_ref[view])

            def chunk(index, carry):
                at = pl.multiple_of(index * CHUNK, CHUNK)
                total = jnp.zeros((CHUNK, row_count), jnp.float32)
                for i, (whole, fraction) in enumerate(steps):
                    here = planes[i, pl.ds(margin + at + whole, CHUNK), :]
                    following = planes[i, pl.ds(margin + at + whole + 1, CHUNK), :]
                    total = total + ((1.0 - fraction) * here + fraction * following)
                partial[view, pl.ds(at, CHUNK), :] = total * weight
                return carry

            lax.fori_loop(0, columns // CHUNK, chunk, 0)

        own_rows = row_count // n
        each = SUBLANES // own_rows
        groups = views // each
        parts = out_ref.shape[0] // groups
        width = columns // parts
        for part in range(parts):
            places = row_places(det_ref, n, each, own_rows, part % 2)
            for group in range(groups):
                moved = 0.0
                for i in range(each):
                    for term in two_terms(partial[group * each + i, part * width : (part + 1) * width, :]):
                        moved = moved + place_dot(places[i], term, ((1,), (1,)))
                out_ref[group * parts + part] = moved.reshape(out_ref.shape[1:])


def backproject_kernel(n, total_depth, view_scale, angle_ref, det_ref, full_ref, out_ref, back):
    views, height, row_count = back.shape
    _, _, columns = out_ref.shape
    layers = pl.num_programs(0)
    margin = (height - columns) // 2
    layer = pl.program_id(0)
    depth = lax.axis_index("gz") * layers - total_depth // 2 + layer

    @pl.when(layer == 0)
    def _():
        own_rows = row_count // n
        each = SUBLANES // own_rows
        groups = views // each
        parts = full_ref.shape[0] // groups
        width = columns // parts
        blank = jnp.zeros((margin, row_count), jnp.float32)
        for view in range(views):
            back[view, :margin, :] = blank
            back[view, margin + columns :, :] = blank
        for part in range(parts):
            places = row_places(det_ref, n, each, own_rows, part % 2)
            for group in range(groups):
                terms = two_terms(full_ref[group * parts + part].reshape(-1, width).T)
                for i in range(each):
                    view = group * each + i
                    moved = place_dot(terms[0], places[i], ((1,), (0,))) + place_dot(
                        terms[1], places[i], ((1,), (0,))
                    )
                    back[view, margin + part * width : margin + (part + 1) * width, :] = moved * (
                        ray_weight(angle_ref[view]) * view_scale
                    )

    steps = [shift_parts(depth, angle_ref[view]) for view in range(views)]

    def chunk(index, carry):
        at = pl.multiple_of(index * LANES, LANES)
        total = jnp.zeros((LANES, row_count), jnp.float32)
        for view, (whole, fraction) in enumerate(steps):
            here = back[view, pl.ds(margin + at - whole, LANES), :]
            before = back[view, pl.ds(margin + at - whole - 1, LANES), :]
            total = total + ((1.0 - fraction) * here + fraction * before)
        out_ref[0, :, pl.ds(at, LANES)] = total.T
        return carry

    lax.fori_loop(0, columns // LANES, chunk, 0)


def exchange_kernel(n, orders, scale, in_ref, meas_ref, res_ref, full_ref,
                    got0, got1, got2, got3, put1, put2, put3, send_sem, recv_sem):
    me = lax.axis_index("gz")
    high_count = n // 8
    core, bit1, bit2, high = me % 2, (me // 2) % 2, (me // 4) % 2, me // 8
    other_core = me + 1 - 2 * core
    other1, other2 = me + 2 - 4 * bit1, me + 4 - 8 * bit2
    others = [me + 8 * (lax.rem(high + j, high_count) - high) for j in range(1, high_count)]
    count = in_ref.shape[0]
    part_columns = in_ref.shape[-1]
    own_rows = meas_ref.shape[1]
    each = SUBLANES // own_rows
    per_group = count * each // meas_ref.shape[0]

    barrier = pltpu.get_barrier_semaphore()
    for peer in [other_core, other1, other2] + others:
        pl.semaphore_signal(barrier, inc=1, device_id={"gz": peer}, device_id_type=MESH)
    pl.semaphore_wait(barrier, 3 + len(others))

    started = {}

    def start(part, stage, source, target, peer):
        copy = pltpu.make_async_remote_copy(
            src_ref=source, dst_ref=target,
            send_sem=send_sem.at[part, stage], recv_sem=recv_sem.at[part, stage],
            device_id={"gz": peer}, device_id_type=MESH,
        )
        copy.start()
        started[part, stage] = copy

    def arrived(part, stage):
        started[part, stage].wait_recv()

    def ends(part):
        if orders[part] == 0:
            return bit1, bit2, other1, other2
        return bit2, bit1, other2, other1

    parts = range(count)
    for part in parts:
        start(part, 0, in_ref.at[part, 1 - core], got0.at[part], other_core)
    for part in parts:
        a, b, peer_a, peer_b = ends(part)
        arrived(part, 0)
        put1[part] = in_ref[part, core, 1 - a] + got0[part, 1 - a]
        start(part, 1, put1.at[part], got1.at[part], peer_a)
    for part in parts:
        a, b, peer_a, peer_b = ends(part)
        arrived(part, 1)
        put2[part] = in_ref[part, core, a, 1 - b] + got0[part, a, 1 - b] + got1[part, 1 - b]
        start(part, 2, put2.at[part], got2.at[part], peer_b)
    for part in parts:
        a, b, peer_a, peer_b = ends(part)
        arrived(part, 2)
        put3[part] = in_ref[part, core, a, b] + got0[part, a, b] + got1[part, b] + got2[part]
        for j, peer in enumerate(others):
            start(part, 3 + j, put3.at[part, lax.rem(high + j + 1, high_count)], got3.at[part, j], peer)
    gather = 3 + len(others)
    for part in parts:
        a, b, peer_a, peer_b = ends(part)
        total = put3[part, high]
        for j in range(len(others)):
            arrived(part, 3 + j)
            total = total + got3[part, j]
        group, column = part // per_group, (part % per_group) * part_columns
        wanted = [meas_ref[group * each + i, :, column : column + part_columns] for i in range(each)]
        residual = (total - jnp.concatenate(wanted, axis=0)) * scale
        for i in range(each):
            res_ref[group * each + i, :, column : column + part_columns] = residual[
                i * own_rows : (i + 1) * own_rows
            ]
        full_ref[part, core, a, b, high] = residual
        mine = full_ref.at[part, core, a, b, high]
        for j, peer in enumerate(others):
            start(part, gather + j, mine, mine, peer)
    last = gather + len(others)
    for part in parts:
        a, b, peer_a, peer_b = ends(part)
        for j in range(len(others)):
            arrived(part, gather + j)
        mine = full_ref.at[part, core, a, b]
        start(part, last, mine, mine, peer_b)
    for part in parts:
        a, b, peer_a, peer_b = ends(part)
        arrived(part, last)
        mine = full_ref.at[part, core, a]
        start(part, last + 1, mine, mine, peer_a)
    for part in parts:
        arrived(part, last + 1)
        mine = full_ref.at[part, core]
        start(part, last + 2, mine, mine, other_core)
    for part in parts:
        arrived(part, last + 2)
    for copy in started.values():
        copy.wait_send()


def per_device(volume, angle_index, detector_rows, measured):
    layers, row_count, columns = volume.shape
    views = angle_index.shape[0]
    n = lax.axis_size("gz")
    total_depth = layers * n
    own_rows = row_count // n
    each = SUBLANES // own_rows
    groups = views // each
    high_count = n // 8
    height = columns + 2 * (total_depth // 2 + SUBLANES)
    part_columns = columns // COLUMN_PARTS
    count = groups * COLUMN_PARTS
    orders = tuple((part % COLUMN_PARTS) % 2 for part in range(count))
    res_scale = total_depth ** (-0.5)
    view_scale = (views * lax.axis_size("vert")) ** (-0.5)
    detectors = detector_rows.reshape(1, row_count)

    smem = pl.BlockSpec(memory_space=pltpu.SMEM)
    vmem = pl.BlockSpec(memory_space=pltpu.VMEM)
    full_shape = (count, 2, 2, 2, high_count, SUBLANES, part_columns)
    half = (SUBLANES, part_columns)
    whole = pl.BlockSpec(full_shape, lambda i: (0,) * len(full_shape))
    one_row = pl.BlockSpec((1, row_count), lambda i: (0, 0))
    plane = pl.BlockSpec((1, row_count, columns), lambda i: (i, 0, 0))
    partials = pl.pallas_call(
        functools.partial(project_kernel, n, total_depth),
        grid=(layers,),
        out_shape=jax.ShapeDtypeStruct(full_shape, jnp.float32),
        in_specs=[smem, one_row, plane],
        out_specs=whole,
        scratch_shapes=[
            pltpu.VMEM((layers, height, row_count), jnp.float32),
            pltpu.VMEM((views, columns, row_count), jnp.float32),
        ],
        name="project",
    )(angle_index, detectors, volume)

    others = high_count - 1
    stages = 6 + 2 * others
    residual, full = pl.pallas_call(
        functools.partial(exchange_kernel, n, orders, res_scale),
        out_shape=(
            jax.ShapeDtypeStruct(measured.shape, jnp.float32),
            jax.ShapeDtypeStruct(full_shape, jnp.float32),
        ),
        in_specs=[vmem, vmem],
        out_specs=(vmem, vmem),
        scratch_shapes=[
            pltpu.VMEM((count, 2, 2, high_count) + half, jnp.float32),
            pltpu.VMEM((count, 2, high_count) + half, jnp.float32),
            pltpu.VMEM((count, high_count) + half, jnp.float32),
            pltpu.VMEM((count, others) + half, jnp.float32),
            pltpu.VMEM((count, 2, high_count) + half, jnp.float32),
            pltpu.VMEM((count, high_count) + half, jnp.float32),
            pltpu.VMEM((count, high_count) + half, jnp.float32),
            pltpu.SemaphoreType.DMA((count, stages)),
            pltpu.SemaphoreType.DMA((count, stages)),
        ],
        compiler_params=pltpu.CompilerParams(collective_id=0, has_side_effects=True),
        name="exchange",
    )(partials, measured)

    gradient = pl.pallas_call(
        functools.partial(backproject_kernel, n, total_depth, view_scale),
        grid=(layers,),
        out_shape=jax.ShapeDtypeStruct((layers, row_count, columns), jnp.float32),
        in_specs=[smem, one_row, whole],
        out_specs=plane,
        scratch_shapes=[pltpu.VMEM((views, height, row_count), jnp.float32)],
        name="backproject",
    )(angle_index, detectors, full)
    gradient = lax.psum_scatter(gradient, "vert", scatter_dimension=1, tiled=True)
    return (residual, gradient)


def solution(mesh):
    in_specs = (P("gz", None, None), P("vert"), P(), P("vert", "gz", None))
    out_specs = (P("vert", "gz", None), P("gz", "vert", None))
    return jax.shard_map(
        per_device, mesh=mesh, in_specs=in_specs, out_specs=out_specs, check_vma=False
    )
```

time: 87.9 us -> 68.8 us (0.78)
  Pallas kernels: 80 us -> 67.1 us
  local copies, waits for them, and re-layouts: 5.42 us -> 0.63 us
  other arithmetic: 1.36 us -> 0 us
    pallas_call x2, Pallas kernels: 35.6 us -> 24.2 us  [the longest x1 12.8 us: per_device(): pl.pallas_call(functools.partial(backproject_kernel, n, total_depth, view...]
    reshape x3 -> x0, local copies, waits for them, and re-layouts: 3.74 us -> none  [the longest x1 1.49 us: per_device(): measured.reshape(groups, SUBLANES, columns)]
    broadcast_in_dim x2 -> x0, local copies, waits for them, and re-layouts: 1.44 us -> none  [the longest x1 0.85 us: per_device(): target[:, :, None]]
    pallas_call x1, Pallas kernels: 44.3 us -> 42.9 us  [per_device(): pl.pallas_call(functools.partial(exchange_kernel, n, orders, res_scale),...]
    mul x2 -> x0, other arithmetic: 1.27 us -> none  [the longest x1 1.26 us: per_device(): weight * view_scale]
where the time goes in v2:
time: 68.8 us; the launch traced here: 68.4 us
  Pallas kernels  67.1 us (98%)
    pallas_call x1, Pallas kernels, per_device(): pl.pallas_call(functools.partial(exchange_kernel, n, orders, res_scale),...  42.9 us
    pallas_call x1, Pallas kernels, per_device(): pl.pallas_call(functools.partial(backproject_kernel, n, total_depth, view...  12.8 us
    pallas_call x1, Pallas kernels, per_device(): pl.pallas_call(functools.partial(project_kernel, n, total_depth), grid=(l...  11.4 us

profile of v2, /device:TPU:1, one launch (start us, length us, event | category | flops | bytes accessed | tf_op | source)
XLA Modules:
  0.0 68.4 jit_solution(2164809231009202642)
XLA Ops:
  0.6 11.4 %project.1.in_ref = f32[4,2,2,2,4,8,512]{6,5,4,3,2,1,0:T(8,128)} custom-call(s32[4]{0:T(128)} %angle_ref.3, s32[1,128]{1,0:T(1,128)} %bitcast.1, f32[8,128,1024]{2,1,0:T(8,128)} %vol_ref.1), custom_call_target="tpu_custom_call" | custom-call | tf_op jit(solution)/shard_map/project/pallas_call | solution.py:282
  12.0 42.9 %exchange.1 = (f32[4,4,1024]{2,1,0:T(4,128)}, f32[4,2,2,2,4,8,512]{6,5,4,3,2,1,0:T(8,128)}) custom-call(f32[4,2,2,2,4,8,512]{6,5,4,3,2,1,0:T(8,128)} %project.1.in_ref, f32[4,4,1024]{2,1,0:T(4,128)} %meas_ref.1), custom_call_target="tpu_custom_call" | custom-call | tf_op jit(solution)/shard_map/exchange/pallas_call | solution.py:297
  55.0 0.0 copy-start
  55.0 12.8 %backproject.1 = f32[8,128,1024]{2,1,0:T(8,128)} custom-call(s32[4]{0:T(128)} %angle_ref.3, s32[1,128]{1,0:T(1,128)} %bitcast.2, f32[4,2,2,2,4,8,512]{6,5,4,3,2,1,0:T(8,128)} %get-tuple-element.5.full_ref), custom_call_target="tpu_custom_call" | custom-call | tf_op jit(solution)/shard_map/backproject/pallas_call | solution.py:320
  67.8 0.0 copy-done
  67.8 0.6 copy.7
Async XLA Ops:
  55.0 12.8 %copy-start = (f32[4,4,1024]{2,1,0:T(4,128)S(1)}, f32[4,4,1024]{2,1,0:T(4,128)}, u32[]{:S(2)}) copy-start(f32[4,4,1024]{2,1,0:T(4,128)} %get-tuple-element.8) | copy-start | bytes 196612

commit v3 on v0

v3 whole, which is shorter than its diff:
```python
import functools

import jax
import jax.numpy as jnp
from jax import lax
from jax.experimental import pallas as pl
from jax.experimental.pallas import tpu as pltpu
from jax.sharding import PartitionSpec as P

ANGLES = 512
LANES = 128
SUBLANES = 8
COLUMN_PARTS = 4
STAGGER = 0.4
VMEM_LIMIT = 36 * 2**20
CHUNK = 64
MESH = pl.DeviceIdType.MESH


def log2(value):
    return value.bit_length() - 1


def shift_parts(depth, angle):
    product = depth * (2 * angle - ANGLES)
    whole = lax.shift_right_arithmetic(product, jnp.int32(log2(ANGLES)))
    fraction = (product - whole * ANGLES).astype(jnp.float32) * (1.0 / ANGLES)
    return whole, fraction


def ray_weight(angle):
    slope = (2 * angle - ANGLES).astype(jnp.float32) * (1.0 / ANGLES)
    return jnp.sqrt(jnp.full((1, LANES), 1.0 + slope * slope, jnp.float32))


def row_places(det_ref, n, each, own_rows, order):
    row_count = det_ref.shape[1]
    count = n * each * own_rows
    place = lax.broadcasted_iota(jnp.int32, (count, row_count), 0)
    detector = lax.broadcasted_iota(jnp.int32, (count, row_count), 1)
    row = place & (own_rows - 1)
    view = lax.shift_right_logical(place, log2(own_rows)) & (each - 1)
    slot = lax.shift_right_logical(place, log2(own_rows * each))
    high_count = n // 8
    high = slot & (high_count - 1)
    bits = lax.shift_right_logical(slot, log2(high_count))
    second, first, core = bits & 1, lax.shift_right_logical(bits, 1) & 1, lax.shift_right_logical(bits, 2)
    bit1, bit2 = (first, second) if order == 0 else (second, first)
    owner = high * 8 + bit2 * 4 + bit1 * 2 + core
    from_detector = (owner * own_rows + row) == detector
    volume_row = lax.broadcasted_iota(jnp.int32, (row_count, row_count), 0)
    records = (det_ref[...] == volume_row).astype(jnp.float32).astype(jnp.bfloat16)
    places = []
    for i in range(each):
        pick = (from_detector & (view == i)).astype(jnp.float32).astype(jnp.bfloat16)
        moved = lax.dot_general(pick, records, (((1,), (1,)), ((), ())), preferred_element_type=jnp.float32)
        places.append(moved.astype(jnp.bfloat16))
    return places


def two_terms(values):
    high = values.astype(jnp.bfloat16)
    return high, (values - high.astype(jnp.float32)).astype(jnp.bfloat16)


def place_dot(a, b, dims):
    return lax.dot_general(a, b, (dims, ((), ())), preferred_element_type=jnp.float32)


def forward_kernel(n, orders, total_depth, scale, view_scale, angle_ref, det_ref, meas_ref, vol_ref,
                   res_ref, back_ref, slabs, planes, places, partial, own, full,
                   got0, got1, got2, got3, put1, put2, put3, load_sem, send_sem, recv_sem):
    layers, height, row_count = planes.shape
    views, own_rows, columns = meas_ref.shape
    margin = (height - columns) // 2
    each = SUBLANES // own_rows
    count, width = own.shape[0], own.shape[-1]
    per_group = count * each // views

    me = lax.axis_index("gz")
    high_count = n // 8
    core, bit1, bit2, high = me % 2, (me // 2) % 2, (me // 4) % 2, me // 8
    other_core = me + 1 - 2 * core
    other1, other2 = me + 2 - 4 * bit1, me + 4 - 8 * bit2
    others = [me + 8 * (lax.rem(high + j, high_count) - high) for j in range(1, high_count)]
    base = me * layers - total_depth // 2

    loads = [
        pltpu.make_async_copy(vol_ref.at[layer], slabs.at[layer], load_sem.at[layer]) for layer in range(layers)
    ]
    for load in loads:
        load.start()
    barrier = pltpu.get_barrier_semaphore()
    for peer in [other_core, other1, other2] + others:
        pl.semaphore_signal(barrier, inc=1, device_id={"gz": peer}, device_id_type=MESH)

    blank = jnp.zeros((margin, row_count), jnp.float32)
    for layer in range(layers):
        planes[layer, :margin, :] = blank
        planes[layer, margin + columns :, :] = blank
    for view in range(views):
        back_ref[view, :margin, :] = blank
        back_ref[view, margin + columns :, :] = blank
    for order in range(2):
        for i, place in enumerate(row_places(det_ref, n, each, own_rows, order)):
            places[order, i] = place
    for layer in range(layers):
        loads[layer].wait()

        def turn(index, carry):
            at = pl.multiple_of(index * LANES, LANES)
            planes[layer, pl.ds(pl.multiple_of(margin + at, SUBLANES), LANES), :] = slabs[layer, :, pl.ds(at, LANES)].T
            return carry

        lax.fori_loop(0, columns // LANES, turn, 0, unroll=True)
    pl.semaphore_wait(barrier, 3 + len(others))

    started = {}
    gather = 3 + len(others)
    last = gather + len(others)

    def start(part, stage, source, target, peer):
        copy = pltpu.make_async_remote_copy(
            src_ref=source, dst_ref=target,
            send_sem=send_sem.at[part, stage], recv_sem=recv_sem.at[part, stage],
            device_id={"gz": peer}, device_id_type=MESH,
        )
        copy.start()
        started[part, stage] = copy

    def arrived(part, stage):
        started[part, stage].wait_recv()

    def project(part):
        group, left = part // per_group, (part % per_group) * width
        moved = 0.0
        for i in range(each):
            angle = angle_ref[group * each + i]
            steps = [shift_parts(base + layer, angle) for layer in range(layers)]
            weight = ray_weight(angle)

            def chunk(index, carry):
                at = pl.multiple_of(index * CHUNK, CHUNK)
                total = jnp.zeros((CHUNK, row_count), jnp.float32)
                for layer, (whole, fraction) in enumerate(steps):
                    first = margin + left + at + whole
                    here = planes[layer, pl.ds(first, CHUNK), :]
                    following = planes[layer, pl.ds(first + 1, CHUNK), :]
                    total = total + ((1.0 - fraction) * here + fraction * following)
                partial[i, pl.ds(at, CHUNK), :] = total * weight
                return carry

            lax.fori_loop(0, width // CHUNK, chunk, 0)
            for term in two_terms(partial[i]):
                moved = moved + place_dot(places[orders[part], i], term, ((1,), (1,)))
        own[part] = moved.reshape(own.shape[1:])

    def place(part):
        group, left = part // per_group, (part % per_group) * width
        terms = two_terms(full[part].reshape(-1, width).T)
        for i in range(each):
            view = group * each + i
            matrix = places[orders[part], i]
            moved = place_dot(terms[0], matrix, ((1,), (0,))) + place_dot(terms[1], matrix, ((1,), (0,)))
            back_ref[view, margin + left : margin + left + width, :] = moved * (
                ray_weight(angle_ref[view]) * view_scale
            )

    def event(part, stage):
        if orders[part] == 0:
            a, b, peer_a, peer_b = bit1, bit2, other1, other2
        else:
            a, b, peer_a, peer_b = bit2, bit1, other2, other1
        if stage == 0:
            project(part)
            start(part, 0, own.at[part, 1 - core], got0.at[part], other_core)
        elif stage == 1:
            arrived(part, 0)
            put1[part] = own[part, core, 1 - a] + got0[part, 1 - a]
            start(part, 1, put1.at[part], got1.at[part], peer_a)
        elif stage == 2:
            arrived(part, 1)
            put2[part] = own[part, core, a, 1 - b] + got0[part, a, 1 - b] + got1[part, 1 - b]
            start(part, 2, put2.at[part], got2.at[part], peer_b)
        elif stage == 3:
            arrived(part, 2)
            put3[part] = own[part, core, a, b] + got0[part, a, b] + got1[part, b] + got2[part]
            for j, peer in enumerate(others):
                start(part, 3 + j, put3.at[part, lax.rem(high + j + 1, high_count)], got3.at[part, j], peer)
        elif stage == 4:
            total = put3[part, high]
            for j in range(len(others)):
                arrived(part, 3 + j)
                total = total + got3[part, j]
            group, column = part // per_group, (part % per_group) * width
            wanted = [meas_ref[group * each + i, :, column : column + width] for i in range(each)]
            residual = (total - jnp.concatenate(wanted, axis=0)) * scale
            full[part, core, a, b, high] = residual
            mine = full.at[part, core, a, b, high]
            for j, peer in enumerate(others):
                start(part, gather + j, mine, mine, peer)
            for i in range(each):
                res_ref[group * each + i, :, column : column + width] = residual[i * own_rows : (i + 1) * own_rows]
        elif stage == 5:
            for j in range(len(others)):
                arrived(part, gather + j)
            mine = full.at[part, core, a, b]
            start(part, last, mine, mine, peer_b)
        elif stage == 6:
            arrived(part, last)
            mine = full.at[part, core, a]
            start(part, last + 1, mine, mine, peer_a)
        elif stage == 7:
            arrived(part, last + 1)
            mine = full.at[part, core]
            start(part, last + 2, mine, mine, other_core)
        else:
            arrived(part, last + 2)
            place(part)

    for stage, part in sorted(
        ((stage, part) for stage in range(9) for part in range(count)),
        key=lambda item: (item[0] + STAGGER * item[1], -item[0]),
    ):
        event(part, stage)
    for copy in started.values():
        copy.wait_send()


def backproject_kernel(total_depth, angle_ref, back_ref, out_ref):
    views, height, row_count = back_ref.shape
    columns = out_ref.shape[2]
    layers = pl.num_programs(0)
    margin = (height - columns) // 2
    depth = lax.axis_index("gz") * layers - total_depth // 2 + pl.program_id(0)
    steps = [shift_parts(depth, angle_ref[view]) for view in range(views)]

    def chunk(index, carry):
        at = pl.multiple_of(index * LANES, LANES)
        total = jnp.zeros((LANES, row_count), jnp.float32)
        for view, (whole, fraction) in enumerate(steps):
            here = back_ref[view, pl.ds(margin + at - whole, LANES), :]
            before = back_ref[view, pl.ds(margin + at - whole - 1, LANES), :]
            total = total + ((1.0 - fraction) * here + fraction * before)
        out_ref[0, :, pl.ds(at, LANES)] = total.T
        return carry

    lax.fori_loop(0, columns // LANES, chunk, 0)


def per_device(volume, angle_index, detector_rows, measured):
    layers, row_count, columns = volume.shape
    views = angle_index.shape[0]
    n = lax.axis_size("gz")
    total_depth = layers * n
    own_rows = row_count // n
    each = SUBLANES // own_rows
    groups = views // each
    high_count = n // 8
    height = columns + 2 * (total_depth // 2 + SUBLANES)
    width = columns // COLUMN_PARTS
    count = groups * COLUMN_PARTS
    orders = tuple((part % COLUMN_PARTS) % 2 for part in range(count))
    res_scale = total_depth ** (-0.5)
    view_scale = (views * lax.axis_size("vert")) ** (-0.5)

    smem = pl.BlockSpec(memory_space=pltpu.SMEM)
    vmem = pl.BlockSpec(memory_space=pltpu.VMEM)
    half = (SUBLANES, width)
    full_shape = (count, 2, 2, 2, high_count) + half
    back_shape = (views, height, row_count)
    others = high_count - 1
    stages = 6 + 2 * others
    residual, back = pl.pallas_call(
        functools.partial(forward_kernel, n, orders, total_depth, res_scale, view_scale),
        out_shape=(
            jax.ShapeDtypeStruct(measured.shape, jnp.float32),
            jax.ShapeDtypeStruct(back_shape, jnp.float32),
        ),
        in_specs=[smem, vmem, vmem, pl.BlockSpec(memory_space=pltpu.HBM)],
        out_specs=(vmem, vmem),
        scratch_shapes=[
            pltpu.VMEM((layers, row_count, columns), jnp.float32),
            pltpu.VMEM((layers, height, row_count), jnp.float32),
            pltpu.VMEM((2, each, n * SUBLANES, row_count), jnp.bfloat16),
            pltpu.VMEM((each, width, row_count), jnp.float32),
            pltpu.VMEM(full_shape, jnp.float32),
            pltpu.VMEM(full_shape, jnp.float32),
            pltpu.VMEM((count, 2, 2, high_count) + half, jnp.float32),
            pltpu.VMEM((count, 2, high_count) + half, jnp.float32),
            pltpu.VMEM((count, high_count) + half, jnp.float32),
            pltpu.VMEM((count, others) + half, jnp.float32),
            pltpu.VMEM((count, 2, high_count) + half, jnp.float32),
            pltpu.VMEM((count, high_count) + half, jnp.float32),
            pltpu.VMEM((count, high_count) + half, jnp.float32),
            pltpu.SemaphoreType.DMA((layers,)),
            pltpu.SemaphoreType.DMA((count, stages)),
            pltpu.SemaphoreType.DMA((count, stages)),
        ],
        compiler_params=pltpu.CompilerParams(
            collective_id=0, has_side_effects=True, vmem_limit_bytes=VMEM_LIMIT
        ),
        name="forward",
    )(angle_index, detector_rows.reshape(1, row_count), measured, volume)

    gradient = pl.pallas_call(
        functools.partial(backproject_kernel, total_depth),
        grid=(layers,),
        out_shape=jax.ShapeDtypeStruct((layers, row_count, columns), jnp.float32),
        in_specs=[smem, vmem],
        out_specs=pl.BlockSpec((1, row_count, columns), lambda i: (i, 0, 0)),
        compiler_params=pltpu.CompilerParams(vmem_limit_bytes=VMEM_LIMIT),
        name="backproject",
    )(angle_index, back)
    gradient = lax.psum_scatter(gradient, "vert", scatter_dimension=1, tiled=True)
    return (residual, gradient)


def solution(mesh):
    in_specs = (P("gz", None, None), P("vert"), P(), P("vert", "gz", None))
    out_specs = (P("vert", "gz", None), P("gz", "vert", None))
    return jax.shard_map(
        per_device, mesh=mesh, in_specs=in_specs, out_specs=out_specs, check_vma=False
    )
```

time: 548 us -> 58.1 us (0.11)
  local copies, waits for them, and re-layouts: 274 us -> 4.96 us
  waiting for transfers between devices: 192 us -> 0 us
  other arithmetic: 57.8 us -> 0 us
  Pallas kernels: 0 us -> 52.4 us
  between operations: 14.1 us -> 0.65 us
  loops' own time: 5.8 us -> 0 us
    gather x193 -> x0, local copies, waits for them, and re-layouts: 193 us -> none
    unnamed x3 -> x0, waiting for transfers between devices: 136 us -> none
    all_gather x1 -> x0, waiting for transfers between devices: 56.4 us -> none  [per_device(): full_rows = lax.all_gather(residual, 'gz', axis=1, tiled=True)]
    pallas_call x0 -> x2, Pallas kernels: none -> 52.4 us  [the longest x1 42.6 us: per_device(): pl.pallas_call(functools.partial(forward_kernel, n, orders, total_depth,...]
    dynamic_update_slice x8 -> x0, local copies, waits for them, and re-layouts: 43.7 us -> none  [per_device(): partial_cols = lax.map(project, angle_index)]
    add x4 -> x0, other arithmetic: 30.1 us -> none  [add_view(): return (running + weight * contrib, None)]
    reduce_sum x4 -> x0, other arithmetic: 17.6 us -> none  [project(): return weight * jnp.sum(contrib, axis=0)]
    scatter x1 -> x0, local copies, waits for them, and re-layouts: 11.8 us -> none  [per_device(): back = jnp.zeros_like(full_rows).at[:, detector_rows, :].set(full_rows)]
  transfers between devices with their start and end apart: 2 -> 0, of which waited for: 2 -> 0; matrix products, arithmetic and copies ran while one was open for 0% -> 0% of each run, Pallas kernels for 0% -> 0%
where the time goes in v3:
time: 58.1 us; the launch traced here: 58 us
  Pallas kernels  52.4 us (90%)
  local copies, waits for them, and re-layouts  4.96 us (9%)
  between operations  0.65 us (1%)
    pallas_call x1, Pallas kernels, per_device(): pl.pallas_call(functools.partial(forward_kernel, n, orders, total_depth,...  42.6 us
    pallas_call x1, Pallas kernels, per_device(): pl.pallas_call(functools.partial(backproject_kernel, total_depth), grid=(...  9.79 us
    unnamed x9, local copies, waits for them, and re-layouts  4.96 us

profile of v3, /device:TPU:1, one launch (start us, length us, event | category | flops | bytes accessed | tf_op | source)
XLA Modules:
  0.0 58.0 jit_solution(843091768625101308)
XLA Ops:
  0.6 0.0 copy-start
  0.6 2.2 %copy-done = f32[8,128,1024]{2,1,0:T(8,128)S(1)} copy-done((f32[8,128,1024]{2,1,0:T(8,128)S(1)}, f32[8,128,1024]{2,1,0:T(8,128)}, u32[]{:S(2)}) %copy-start) | copy-done | bytes 4194328
  2.8 0.0 copy-start.1
  2.8 0.8 %copy-done.1 = f32[4,4,1024]{2,1,0:T(4,128)S(1)} copy-done((f32[4,4,1024]{2,1,0:T(4,128)S(1)}, f32[4,4,1024]{2,1,0:T(4,128)}, u32[]{:S(2)}) %copy-start.1) | copy-done | bytes 65560
  3.7 0.0 copy-start.2
  3.7 0.7 %copy-done.2 = s32[4]{0:T(128)S(1)} copy-done((s32[4]{0:T(128)S(1)}, s32[4]{0:T(128)}, u32[]{:S(2)}) %copy-start.2) | copy-done | bytes 40
  4.3 0.0 copy-start.3
  4.3 0.7 %copy-done.3 = s32[128]{0:T(128)S(1)} copy-done((s32[128]{0:T(128)S(1)}, s32[128]{0:T(128)}, u32[]{:S(2)}) %copy-start.3) | copy-done | bytes 536
  5.0 42.6 %forward.1 = (f32[4,4,1024]{2,1,0:T(4,128)S(1)}, f32[4,1296,128]{2,1,0:T(8,128)S(1)}) custom-call(s32[4]{0:T(128)S(1)} %copy-done.2, s32[1,128]{1,0:T(1,128)S(1)} %bitcast.1, f32[4,4,1024]{2,1,0:T(4,128)S(1)} %copy-done.1, f32[8,128,1024]{2,1,0:T(8,128)S(1)} %copy-done), custom_call_target="tpu_custom_call" | custom-call | tf_op jit(solution)/shard_map/forward/pallas_call | solution.py:274
  47.6 9.8 %backproject.1 = f32[8,128,1024]{2,1,0:T(8,128)} custom-call(s32[4]{0:T(128)S(1)} %copy-done.2, f32[4,1296,128]{2,1,0:T(8,128)S(1)} %get-tuple-element.5.back_ref), custom_call_target="tpu_custom_call" | custom-call | tf_op jit(solution)/shard_map/backproject/pallas_call | solution.py:306
  57.4 0.6 %copy.7 = f32[4,4,1024]{2,1,0:T(4,128)} copy(f32[4,4,1024]{2,1,0:T(4,128)S(1)} %get-tuple-element.8) | data formatting | bytes 131072
Async XLA Ops:
  0.6 2.2 %copy-start = (f32[8,128,1024]{2,1,0:T(8,128)S(1)}, f32[8,128,1024]{2,1,0:T(8,128)}, u32[]{:S(2)}) copy-start(f32[8,128,1024]{2,1,0:T(8,128)} %vol_ref.1) | copy-start | bytes 12582916
  2.8 0.8 %copy-start.1 = (f32[4,4,1024]{2,1,0:T(4,128)S(1)}, f32[4,4,1024]{2,1,0:T(4,128)}, u32[]{:S(2)}) copy-start(f32[4,4,1024]{2,1,0:T(4,128)} %meas_ref.1) | copy-start | bytes 196612
  3.7 0.7 %copy-start.2 = (s32[4]{0:T(128)S(1)}, s32[4]{0:T(128)}, u32[]{:S(2)}) copy-start(s32[4]{0:T(128)} %angle_ref.3) | copy-start | bytes 52
  4.3 0.7 %copy-start.3 = (s32[128]{0:T(128)S(1)}, s32[128]{0:T(128)}, u32[]{:S(2)}) copy-start(s32[128]{0:T(128)} %param.6) | copy-start | bytes 1540

commit v4 on v3

--- a/solution.py
+++ b/solution.py
@@ -13,6 +13,7 @@
 COLUMN_PARTS = 4
 STAGGER = 0.4
 VMEM_LIMIT = 36 * 2**20
+FORWARD_LIMIT = 58 * 2**20
 CHUNK = 64
 MESH = pl.DeviceIdType.MESH
 
@@ -75,7 +76,6 @@
     margin = (height - columns) // 2
     each = SUBLANES // own_rows
     count, width = own.shape[0], own.shape[-1]
-    per_group = count * each // views
 
     me = lax.axis_index("gz")
     high_count = n // 8
@@ -85,8 +85,14 @@
     others = [me + 8 * (lax.rem(high + j, high_count) - high) for j in range(1, high_count)]
     base = me * layers - total_depth // 2
 
+    groups = views // each
+    slab_count = count // groups
+    reach = -(-(total_depth // 2 + 1) // width)
     loads = [
-        pltpu.make_async_copy(vol_ref.at[layer], slabs.at[layer], load_sem.at[layer]) for layer in range(layers)
+        pltpu.make_async_copy(
+            vol_ref.at[:, :, slab * width : (slab + 1) * width], slabs.at[slab], load_sem.at[slab]
+        )
+        for slab in range(slab_count)
     ]
     for load in loads:
         load.start()
@@ -104,16 +110,19 @@
     for order in range(2):
         for i, place in enumerate(row_places(det_ref, n, each, own_rows, order)):
             places[order, i] = place
-    for layer in range(layers):
-        loads[layer].wait()
-
-        def turn(index, carry):
-            at = pl.multiple_of(index * LANES, LANES)
-            planes[layer, pl.ds(pl.multiple_of(margin + at, SUBLANES), LANES), :] = slabs[layer, :, pl.ds(at, LANES)].T
+    turned = []
+
+    def turn(slab):
+        loads[slab].wait()
+
+        def one(layer, carry):
+            for column in range(0, width, LANES):
+                at = margin + slab * width + column
+                planes[layer, at : at + LANES, :] = slabs[slab, layer, :, column : column + LANES].T
             return carry
 
-        lax.fori_loop(0, columns // LANES, turn, 0, unroll=True)
-    pl.semaphore_wait(barrier, 3 + len(others))
+        lax.fori_loop(0, layers, one, 0, unroll=2)
+        turned.append(slab)
 
     started = {}
     gather = 3 + len(others)
@@ -132,7 +141,7 @@
         started[part, stage].wait_recv()
 
     def project(part):
-        group, left = part // per_group, (part % per_group) * width
+        group, left = part % groups, (part // groups) * width
         moved = 0.0
         for i in range(each):
             angle = angle_ref[group * each + i]
@@ -156,7 +165,7 @@
         own[part] = moved.reshape(own.shape[1:])
 
     def place(part):
-        group, left = part // per_group, (part % per_group) * width
+        group, left = part % groups, (part // groups) * width
         terms = two_terms(full[part].reshape(-1, width).T)
         for i in range(each):
             view = group * each + i
@@ -172,7 +181,11 @@
         else:
             a, b, peer_a, peer_b = bit2, bit1, other2, other1
         if stage == 0:
+            while len(turned) < min(slab_count, part // groups + reach + 1):
+                turn(len(turned))
             project(part)
+            if part == 0:
+                pl.semaphore_wait(barrier, 3 + len(others))
             start(part, 0, own.at[part, 1 - core], got0.at[part], other_core)
         elif stage == 1:
             arrived(part, 0)
@@ -192,7 +205,7 @@
             for j in range(len(others)):
                 arrived(part, 3 + j)
                 total = total + got3[part, j]
-            group, column = part // per_group, (part % per_group) * width
+            group, column = part % groups, (part // groups) * width
             wanted = [meas_ref[group * each + i, :, column : column + width] for i in range(each)]
             residual = (total - jnp.concatenate(wanted, axis=0)) * scale
             full[part, core, a, b, high] = residual
@@ -245,7 +258,7 @@
         out_ref[0, :, pl.ds(at, LANES)] = total.T
         return carry
 
-    lax.fori_loop(0, columns // LANES, chunk, 0)
+    lax.fori_loop(0, columns // LANES, chunk, 0, unroll=True)
 
 
 def per_device(volume, angle_index, detector_rows, measured):
@@ -260,7 +273,7 @@
     height = columns + 2 * (total_depth // 2 + SUBLANES)
     width = columns // COLUMN_PARTS
     count = groups * COLUMN_PARTS
-    orders = tuple((part % COLUMN_PARTS) % 2 for part in range(count))
+    orders = tuple(part % 2 for part in range(count))
     res_scale = total_depth ** (-0.5)
     view_scale = (views * lax.axis_size("vert")) ** (-0.5)
 
@@ -280,7 +293,7 @@
         in_specs=[smem, vmem, vmem, pl.BlockSpec(memory_space=pltpu.HBM)],
         out_specs=(vmem, vmem),
         scratch_shapes=[
-            pltpu.VMEM((layers, row_count, columns), jnp.float32),
+            pltpu.VMEM((COLUMN_PARTS, layers, row_count, width), jnp.float32),
             pltpu.VMEM((layers, height, row_count), jnp.float32),
             pltpu.VMEM((2, each, n * SUBLANES, row_count), jnp.bfloat16),
             pltpu.VMEM((each, width, row_count), jnp.float32),
@@ -293,12 +306,12 @@
             pltpu.VMEM((count, 2, high_count) + half, jnp.float32),
             pltpu.VMEM((count, high_count) + half, jnp.float32),
             pltpu.VMEM((count, high_count) + half, jnp.float32),
-            pltpu.SemaphoreType.DMA((layers,)),
+            pltpu.SemaphoreType.DMA((COLUMN_PARTS,)),
             pltpu.SemaphoreType.DMA((count, stages)),
             pltpu.SemaphoreType.DMA((count, stages)),
         ],
         compiler_params=pltpu.CompilerParams(
-            collective_id=0, has_side_effects=True, vmem_limit_bytes=VMEM_LIMIT
+            collective_id=0, has_side_effects=True, vmem_limit_bytes=FORWARD_LIMIT
         ),
         name="forward",
     )(angle_index, detector_rows.reshape(1, row_count), measured, volume)

time: 58.1 us -> 54.1 us (0.931)
  local copies, waits for them, and re-layouts: 4.96 us -> 2.38 us
  Pallas kernels: 52.4 us -> 50.8 us
    pallas_call x1, Pallas kernels: 9.79 us -> 6.11 us  [per_device(): pl.pallas_call(functools.partial(backproject_kernel, total_depth), grid=(...]
    unnamed x9 -> x7, local copies, waits for them, and re-layouts: 4.96 us -> 2.38 us
    pallas_call x1, Pallas kernels: 42.6 us -> 44.6 us  [per_device(): pl.pallas_call(functools.partial(forward_kernel, n, orders, total_depth,...]
where the time goes in v4:
time: 54.1 us; the launch traced here: 53.8 us
  Pallas kernels  50.8 us (94%)
  local copies, waits for them, and re-layouts  2.38 us (4%)
  between operations  0.66 us (1%)
    pallas_call x1, Pallas kernels, per_device(): pl.pallas_call(functools.partial(forward_kernel, n, orders, total_depth,...  44.6 us
    pallas_call x1, Pallas kernels, per_device(): pl.pallas_call(functools.partial(backproject_kernel, total_depth), grid=(...  6.11 us
    unnamed x7, local copies, waits for them, and re-layouts  2.38 us

profile of v4, /device:TPU:1, one launch (start us, length us, event | category | flops | bytes accessed | tf_op | source)
XLA Modules:
  0.0 53.8 jit_solution(18346480097344644109)
XLA Ops:
  0.6 0.0 copy-start.1
  0.6 44.6 %forward.1 = (f32[4,4,1024]{2,1,0:T(4,128)}, f32[4,1296,128]{2,1,0:T(8,128)}) custom-call(s32[4]{0:T(128)} %angle_ref.3, s32[1,128]{1,0:T(1,128)} %bitcast.1, f32[4,4,1024]{2,1,0:T(4,128)} %meas_ref.1, f32[8,128,1024]{2,1,0:T(8,128)} %vol_ref.1), custom_call_target="tpu_custom_call" | custom-call | tf_op jit(solution)/shard_map/forward/pallas_call | solution.py:287
  45.3 0.0 copy-done.1
  45.3 0.0 copy-start
  45.3 1.7 %copy-done = f32[4,1296,128]{2,1,0:T(8,128)S(1)} copy-done((f32[4,1296,128]{2,1,0:T(8,128)S(1)}, f32[4,1296,128]{2,1,0:T(8,128)}, u32[]{:S(2)}) %copy-start) | copy-done | bytes 2654232
  47.1 0.0 copy-start.2
  47.1 6.1 %backproject.1 = f32[8,128,1024]{2,1,0:T(8,128)} custom-call(s32[4]{0:T(128)S(1)} %copy-done.1, f32[4,1296,128]{2,1,0:T(8,128)S(1)} %copy-done), custom_call_target="tpu_custom_call" | custom-call | tf_op jit(solution)/shard_map/backproject/pallas_call | solution.py:319
  53.2 0.0 copy-done.2
  53.2 0.6 %copy.7 = f32[4,4,1024]{2,1,0:T(4,128)} copy(f32[4,4,1024]{2,1,0:T(4,128)S(1)} %copy-done.2) | data formatting | bytes 131072
Async XLA Ops:
  0.6 44.7 %copy-start.1 = (s32[4]{0:T(128)S(1)}, s32[4]{0:T(128)}, u32[]{:S(2)}) copy-start(s32[4]{0:T(128)} %angle_ref.3) | copy-start | bytes 52
  45.3 1.8 %copy-start = (f32[4,1296,128]{2,1,0:T(8,128)S(1)}, f32[4,1296,128]{2,1,0:T(8,128)}, u32[]{:S(2)}) copy-start(f32[4,1296,128]{2,1,0:T(8,128)} %get-tuple-element.5.back_ref) | copy-start | bytes 7962628
  47.1 6.1 %copy-start.2 = (f32[4,4,1024]{2,1,0:T(4,128)S(1)}, f32[4,4,1024]{2,1,0:T(4,128)}, u32[]{:S(2)}) copy-start(f32[4,4,1024]{2,1,0:T(4,128)} %get-tuple-element.8) | copy-start | bytes 196612

commit v5 on v4

--- a/solution.py
+++ b/solution.py
@@ -11,9 +11,9 @@
 LANES = 128
 SUBLANES = 8
 COLUMN_PARTS = 4
-STAGGER = 0.4
+STAGGER = 0.35
 VMEM_LIMIT = 36 * 2**20
-FORWARD_LIMIT = 58 * 2**20
+FORWARD_LIMIT = 50 * 2**20
 CHUNK = 64
 MESH = pl.DeviceIdType.MESH
 

time: 54.1 us -> 52.2 us (0.965)
  Pallas kernels: 50.8 us -> 48.6 us
    pallas_call x1, Pallas kernels: 44.6 us -> 42.3 us  [per_device(): pl.pallas_call(functools.partial(forward_kernel, n, orders, total_depth,...]
where the time goes in v5:
time: 52.2 us; the launch traced here: 52.1 us
  Pallas kernels  48.6 us (93%)
  local copies, waits for them, and re-layouts  2.77 us (5%)
  between operations  0.65 us (1%)
    pallas_call x1, Pallas kernels, per_device(): pl.pallas_call(functools.partial(forward_kernel, n, orders, total_depth,...  42.3 us
    pallas_call x1, Pallas kernels, per_device(): pl.pallas_call(functools.partial(backproject_kernel, total_depth), grid=(...  6.36 us
    unnamed x7, local copies, waits for them, and re-layouts  2.77 us

profile of v5, /device:TPU:1, one launch (start us, length us, event | category | flops | bytes accessed | tf_op | source)
XLA Modules:
  0.0 52.1 jit_solution(15278697665745768384)
XLA Ops:
  0.6 0.0 copy-start
  0.6 0.8 %copy-done = f32[4,4,1024]{2,1,0:T(4,128)S(1)} copy-done((f32[4,4,1024]{2,1,0:T(4,128)S(1)}, f32[4,4,1024]{2,1,0:T(4,128)}, u32[]{:S(2)}) %copy-start) | copy-done | bytes 65560
  1.5 0.0 copy-start.1
  1.5 0.7 %copy-done.1 = s32[4]{0:T(128)S(1)} copy-done((s32[4]{0:T(128)S(1)}, s32[4]{0:T(128)}, u32[]{:S(2)}) %copy-start.1) | copy-done | bytes 40
  2.1 0.0 copy-start.2
  2.1 0.7 %copy-done.2 = s32[128]{0:T(128)S(1)} copy-done((s32[128]{0:T(128)S(1)}, s32[128]{0:T(128)}, u32[]{:S(2)}) %copy-start.2) | copy-done | bytes 536
  2.8 42.3 %forward.1 = (f32[4,4,1024]{2,1,0:T(4,128)S(1)}, f32[4,1296,128]{2,1,0:T(8,128)S(1)}) custom-call(s32[4]{0:T(128)S(1)} %copy-done.1, s32[1,128]{1,0:T(1,128)S(1)} %bitcast.1, f32[4,4,1024]{2,1,0:T(4,128)S(1)} %copy-done, f32[8,128,1024]{2,1,0:T(8,128)} %vol_ref.1), custom_call_target="tpu_custom_call" | custom-call | tf_op jit(solution)/shard_map/forward/pallas_call | solution.py:287
  45.1 6.4 %backproject.1 = f32[8,128,1024]{2,1,0:T(8,128)} custom-call(s32[4]{0:T(128)S(1)} %copy-done.1, f32[4,1296,128]{2,1,0:T(8,128)S(1)} %get-tuple-element.5.back_ref), custom_call_target="tpu_custom_call" | custom-call | tf_op jit(solution)/shard_map/backproject/pallas_call | solution.py:319
  51.4 0.6 %copy.7 = f32[4,4,1024]{2,1,0:T(4,128)} copy(f32[4,4,1024]{2,1,0:T(4,128)S(1)} %get-tuple-element.8) | data formatting | bytes 131072
Async XLA Ops:
  0.6 0.8 %copy-start = (f32[4,4,1024]{2,1,0:T(4,128)S(1)}, f32[4,4,1024]{2,1,0:T(4,128)}, u32[]{:S(2)}) copy-start(f32[4,4,1024]{2,1,0:T(4,128)} %meas_ref.1) | copy-start | bytes 196612
  1.5 0.7 %copy-start.1 = (s32[4]{0:T(128)S(1)}, s32[4]{0:T(128)}, u32[]{:S(2)}) copy-start(s32[4]{0:T(128)} %angle_ref.3) | copy-start | bytes 52
  2.1 0.7 %copy-start.2 = (s32[128]{0:T(128)S(1)}, s32[128]{0:T(128)}, u32[]{:S(2)}) copy-start(s32[128]{0:T(128)} %param.6) | copy-start | bytes 1540
